TPU v7x, 32 devices: a whole 2x2x4 slice. The times are simulated.
32 devices in a mesh: dp: 4 (over y, core), seq: 2 (over x), expert: 4 (over z).
Axes of the slice: x: 2, y: 2, z: 4, core: 2. Of those that a mesh axis runs over, the one named last changes fastest.
Arguments:
- queries: bfloat16 [512, 4096], P(('dp', 'seq'), 'expert'), parts along dimension 0, may hold values from -256 to 256, as said below
- keys: bfloat16 [2048, 1024], P(('dp', 'seq'), 'expert'), parts along dimension 0, may hold values from -6 to 6
- values: bfloat16 [2048, 1024], P(('dp', 'seq'), 'expert'), parts along dimension 0, may hold values from -6 to 6
- lengths: int32 [32], P('dp'), parts along dimension 0, may hold values from 1 to 256, 512 in all
- routes: int32 [512, 2], P(('dp', 'seq', 'expert')), parts along dimension 0, may hold values from 0 to 3, all different within a row; in each aligned block of 16 rows (0 to 15, 16 to 31, ...) at most 12 rows name the same one
- gates: float32 [512, 2], P(('dp', 'seq', 'expert')), parts along dimension 0, may hold values from 0.2 to 1
- w_up: bfloat16 [4, 4096, 7168], P('expert', None, 'seq'), may hold values from -0.09375 to 0.09375
Outputs:
- expert_mix: bfloat16 [512, 7168], P(('dp', 'seq', 'expert')), parts along dimension 0
There are 4 independent parts, one for each index of `dp`. A program takes and returns all parts, laid end to end along the dimension named above; an argument that names none is the same for every part. Nothing has to cross between parts.
Inputs may be any that keep to these rules, and one draw needn't show every extreme that they name: `queries`: A query row's values are those of a normal draw or, in some rows, a multiple of a sum of key rows. The 8 lengths sum to 512. `routes`: A row's two experts differ; among the 16 rows of one device no expert is named more than 12 times.
All inputs are finite; a program needn't handle non-finite values.
Results may differ from a plain program's by a relative error of at most 0.012.
Values may be sent and summed in bfloat16 or wider, within the bound.
A program may use at most 64 MiB of HBM per device.

v0:
```python
import functools

import jax
import jax.numpy as jnp
from jax import lax
from jax.experimental import pallas as pl
from jax.experimental.pallas import tpu as pltpu
from jax.sharding import PartitionSpec as P

HD = 128
MESH = pl.DeviceIdType.MESH
F32 = jnp.float32
BF16 = jnp.bfloat16
NT = (((1,), (1,)), ((), ()))


def up(n, m):
    return -(-n // m) * m


def iota(shape, dim):
    return lax.broadcasted_iota(jnp.int32, shape, dim)


def onehot(mask):
    return jnp.where(mask, F32(1.0), F32(0.0)).astype(BF16)


def dot(a, b):
    return jnp.dot(a, b, preferred_element_type=F32)


def kernel(
    cfg,
    len_hbm, q_hbm, k_hbm, v_hbm, routes_hbm, gates_hbm, w_hbm, out_hbm,
    len_ref, q_ref, k_ref, v_ref, routes_ref, gates_ref, out_ref,
    wbuf, kbuf, vbuf, rbuf, pack, xbuf, acc, sendbuf, recv,
    in_sem, w_sem, kv_send, kv_recv, r_send, r_recv, z_send, z_recv, x_send, x_recv,
    own_sem, b_send, b_recv, out_sem,
):
    S, E, ndoc, cap, RB, F, RP, nc, steps, pieces, tile = cfg
    s = lax.axis_index("seq")
    e = lax.axis_index("expert")
    q_rows, width = q_ref.shape
    shard = k_ref.shape[0]
    kvl = k_ref.shape[1] // HD
    group = width // HD // kvl
    T = routes_ref.shape[1]
    ff = w_hbm.shape[1]
    depth = w_hbm.shape[0]
    scale = 1.0 / HD**0.5

    def at_s(d):
        return lax.rem(s + S - d, S)

    def at_e(d):
        return lax.rem(e + E - d, E)

    barrier = pltpu.get_barrier_semaphore()
    for ds in range(S):
        for de in range(E):
            if ds or de:
                pl.semaphore_signal(
                    barrier, inc=1, device_id={"seq": at_s(ds), "expert": at_e(de)},
                    device_id_type=MESH,
                )

    def w_copy(r):
        src = lax.rem(e + r, E)
        return pltpu.make_async_copy(
            w_hbm.at[pl.ds(pl.multiple_of(src * width, width), width)], wbuf.at[r], w_sem.at[r]
        )

    ins = []
    for i, (src, dst) in enumerate((
        (k_hbm, k_ref), (v_hbm, v_ref), (routes_hbm, routes_ref), (q_hbm, q_ref),
        (len_hbm, len_ref), (gates_hbm, gates_ref),
    )):
        c = pltpu.make_async_copy(src, dst, in_sem.at[i])
        c.start()
        ins.append(c)
    for c in ins[:3]:
        c.wait()
    pl.semaphore_wait(barrier, S * E - 1)

    def remote(src, dst, ssem, rsem, ds, de):
        return pltpu.make_async_remote_copy(
            src_ref=src, dst_ref=dst, send_sem=ssem, recv_sem=rsem,
            device_id={"seq": at_s(ds), "expert": at_e(de)}, device_id_type=MESH,
        )

    kv_copies = []
    offset = 0
    for i, (d, first) in enumerate(pieces):
        n = shard - first
        kc = remote(k_ref.at[pl.ds(first, n)], kbuf.at[pl.ds(offset, n)],
                    kv_send.at[2 * i], kv_recv.at[2 * i], S - d, 0)
        vc = remote(v_ref.at[pl.ds(first, n)], vbuf.at[pl.ds(offset, n)],
                    kv_send.at[2 * i + 1], kv_recv.at[2 * i + 1], S - d, 0)
        kc.start()
        vc.start()
        kv_copies += [kc, vc]
        offset += n
    r_copies = []
    for de in range(1, E):
        c = remote(routes_ref, rbuf.at[de], r_send.at[de], r_recv.at[de], 0, de)
        c.start()
        r_copies.append(c)

    for c in ins[3:]:
        c.wait()
    for r in range(E):
        w_copy(r).start()
    qn = group * q_rows
    qpos = s * shard + shard - q_rows + lax.rem(iota((qn, 1), 0), q_rows)
    docstart = jnp.zeros((qn, 1), jnp.int32)
    begin = jnp.int32(0)
    for j in range(ndoc):
        docstart = jnp.where(qpos >= begin, begin, docstart)
        begin = begin + len_ref[j]

    def masked(q, k, first):
        sc = lax.dot_general(q, k, NT, preferred_element_type=F32) * scale
        kpos = first + iota((1, k.shape[0]), 1)
        return jnp.where((kpos <= qpos) & (kpos >= docstart), sc, F32(-1e30))

    queries = []
    local = []
    for h in range(kvl):
        q = jnp.concatenate(
            [q_ref[:, (h * group + g) * HD:(h * group + g + 1) * HD] for g in range(group)], axis=0
        )
        queries.append(q)
        sc = masked(q, k_ref[:, h * HD:(h + 1) * HD], s * shard)
        peak = jnp.max(sc, axis=-1, keepdims=True)
        wt = jnp.exp(sc - peak)
        local.append((peak, jnp.sum(wt, axis=-1, keepdims=True),
                      dot(wt.astype(BF16), v_ref[:, h * HD:(h + 1) * HD])))

    for c in r_copies:
        c.wait()
    mine = routes_ref[...]
    names = iota((up(E, 8), 1), 0)

    def members(rt):
        return onehot((rt[0:1, :] == names) | (rt[1:2, :] == names))

    upper = onehot(iota((T, T), 0) < iota((T, T), 1))
    blocks = []
    for de in range(E):
        mt = members(mine if de == 0 else rbuf[de])
        cnt = dot(mt, upper)
        blk = lax.rem(e + de, E)
        place = jnp.where(mt > 0.5, cnt + (blk * cap).astype(F32), F32(-1.0))
        blocks.append((place, blk))
        if de == 0:
            before = cnt
    Q = q_rows
    total_place = jnp.zeros((up(E, 8), Q), F32)
    for place, blk in blocks:
        shift = onehot(iota((T, Q), 0) + blk * T == iota((T, Q), 1))
        total_place = total_place + dot((place + 1.0).astype(BF16), shift)
    row_of = iota((RB, Q), 0).astype(F32) + 1.0
    sel = []
    for x in range(E):
        sel.append(onehot(total_place[x:x + 1, :] == row_of))
    selector = jnp.concatenate(sel, axis=0)

    for c in kv_copies:
        c.wait()
    hw = group * HD
    z_copies, x_copies, own_copies = {}, {}, []

    def relay(r, h, src):
        for ds in range(1, S):
            c = remote(src, xbuf.at[S - ds, r, :, pl.ds(h * hw, hw)],
                       x_send.at[h, r, ds], x_recv.at[h, r, S - ds], ds, 0)
            c.start()
            x_copies[h, r, ds] = c

    def send_head(h):
        part = pl.ds(h * hw, hw)
        for r in range(1, E):
            c = remote(pack.at[at_e(r), :, part], xbuf.at[0, r, :, part],
                       z_send.at[h, r], z_recv.at[h, r], 0, r)
            c.start()
            z_copies[h, r] = c
        relay(0, h, pack.at[e, :, part])
        own = pltpu.make_async_copy(pack.at[e, :, part], xbuf.at[0, 0, :, part], own_sem.at[h])
        own.start()
        own_copies.append(own)

    for h in range(kvl):
        q = queries[h]
        hs = slice(h * HD, (h + 1) * HD)
        peak, total, got = local[h]
        offset = 0
        for d, first in pieces:
            n = shard - first
            sc = masked(q, kbuf[offset:offset + n, hs], (s - d) * shard + first)
            higher = jnp.maximum(peak, jnp.max(sc, axis=-1, keepdims=True))
            wt = jnp.exp(sc - higher)
            fade = jnp.exp(peak - higher)
            total = total * fade + jnp.sum(wt, axis=-1, keepdims=True)
            got = got * fade + dot(wt.astype(BF16), vbuf[offset:offset + n, hs])
            peak = higher
            offset += n
        att = (got / total).astype(BF16)
        for g in range(group):
            cols = slice((h * group + g) * HD, (h * group + g + 1) * HD)
            packed = dot(selector, att[g * q_rows:(g + 1) * q_rows]).astype(BF16)
            for x in range(E):
                pack[x, :, cols] = packed[x * RB:(x + 1) * RB]
        send_head(h)

    rows_out, rows_in = E * RP, F * RB
    out_row = iota((rows_out, 1), 0)
    inner = lax.rem(out_row, RP)
    e_of = lax.rem(e + E - lax.div(out_row, RP), E)
    from_row = lax.div(inner, cap) * RB + e_of * cap + lax.rem(inner, cap)
    from_row = jnp.where(inner < F * cap, from_row, -1)
    perm = onehot(from_row == iota((rows_out, rows_in), 1))

    diagonal = iota((T, T), 0) == iota((T, T), 1)

    def column(row):
        return jnp.sum(jnp.where(diagonal, row, jnp.zeros_like(row)), axis=1, keepdims=True)

    picks = []
    wide = iota((T, E * RP), 1)
    at = []
    for k in range(2):
        rk = mine[k:k + 1, :]
        slot = jnp.sum(jnp.where(rk == names, before, F32(0.0)), axis=0, keepdims=True)
        rel = rk - e
        rel = jnp.where(rel < 0, rel + E, rel)
        at.append(column((rel * RP).astype(F32) + slot).astype(jnp.int32))
    for f in range(F):
        for k in range(2):
            picks.append(onehot(at[k] + f * cap == wide))
    pick = jnp.concatenate(picks, axis=0)

    sends = {}

    def squares(g, r):
        xf = xbuf[g, r].astype(F32)
        return jnp.sum(xf * xf, axis=-1, keepdims=True)

    def give_back(g, square, product):
        factor = lax.rsqrt(square / depth + 1e-05)
        for st, (c0, n) in enumerate(steps):
            folded = []
            for f in range(F):
                part = product(slice(f * nc + c0, f * nc + c0 + n)) * factor
                folded.append((part / (1.0 + jnp.exp(-part))).astype(BF16))
            moved = dot(perm, jnp.concatenate(folded, axis=0)).astype(BF16)
            for de in range(E):
                block = moved[de * RP:(de + 1) * RP]
                if g or de:
                    sendbuf[de, g, :, c0:c0 + n] = block
                else:
                    recv[0, 0, :, c0:c0 + n] = block
            for de in reversed(range(E)):
                if g or de:
                    c = remote(sendbuf.at[de, g, :, pl.ds(c0, n)],
                               recv.at[g, de, :, pl.ds(c0, n)],
                               b_send.at[st, de, g], b_recv.at[st, de, g], g, de)
                    c.start()
                    sends[st, de, g] = c

    square = jnp.zeros((RB, 1), F32)
    for r in range(E):
        for h in range(kvl):
            if r:
                z_copies[h, r].wait()
                relay(r, h, xbuf.at[0, r, :, pl.ds(h * hw, hw)])
            else:
                own_copies[h].wait()
        w_copy(r).wait()
        square = square + squares(0, r)
        x = xbuf[0, r]
        if r < E - 1:
            def body(i, carry, r=r, x=x):
                cols = pl.ds(pl.multiple_of(i * tile, tile), tile)
                part = dot(x, wbuf[r, :, cols])
                if r == 0:
                    acc[:, cols] = part
                else:
                    acc[:, cols] += part
                return carry

            lax.fori_loop(0, ff // tile, body, 0)
        else:
            def last(cols, r=r, x=x):
                part = dot(x, wbuf[r, :, cols])
                return part + acc[:, cols] if r else part

            give_back(0, square, last)
    for g in range(1, S):
        square = jnp.zeros((RB, 1), F32)
        for r in range(E):
            for h in range(kvl):
                x_copies[h, r, S - g].wait_recv()
            square = square + squares(g, r)

        def whole(cols, g=g):
            part = dot(xbuf[g, 0], wbuf[0, :, cols])
            for r in range(1, E):
                part = part + dot(xbuf[g, r], wbuf[r, :, cols])
            return part

        give_back(g, square, whole)
    for c in x_copies.values():
        c.wait_send()

    g0, g1 = column(gates_ref[0:1, :]), column(gates_ref[1:2, :])
    outs = []
    for g in range(S):
        base = pl.multiple_of(lax.rem(s + g, S) * ff, 128)
        for st, (c0, n) in enumerate(steps):
            for de in range(E):
                if g or de:
                    sends[st, de, g].wait()
            got = recv[g, :, :, c0:c0 + n].reshape(E * RP, n)
            res = dot(pick, got)
            for f in range(F):
                lo = 2 * f * T
                mix = g0 * res[lo:lo + T] + g1 * res[lo + T:lo + 2 * T]
                cols = slice(f * nc + c0, f * nc + c0 + n)
                out_ref[g, :, cols] = mix.astype(BF16)
        c = pltpu.make_async_copy(out_ref.at[g], out_hbm.at[:, pl.ds(base, ff)], out_sem.at[g])
        c.start()
        outs.append(c)
    for c in outs:
        c.wait()


def shards(queries, keys, values, lengths, routes, gates, w_up):
    S, E = lax.axis_size("seq"), lax.axis_size("expert")
    q_rows, width = queries.shape
    shard = keys.shape[0]
    w = w_up.reshape(w_up.shape[1], w_up.shape[2])
    depth, ff = w.shape
    T = routes.shape[0]
    cap = max(2, 3 * q_rows // (E * E))
    RB = up(E * cap, 16)
    choices = [f for f in range(1, ff // 128 + 1) if ff % (f * 128) == 0]
    F = min(choices, key=lambda f: up(f * cap, 16) * (ff // f))
    RP = up(F * cap, 16)
    nc = ff // F
    cuts = list(range(0, max(nc - 255, 1), 256))
    steps = [(c, (cuts + [nc])[i + 1] - c) for i, c in enumerate(cuts)]
    tile = 512 if ff % 512 == 0 else 128
    window = shard * S // 2
    pieces = []
    for d in range(1, S):
        first = max(0, (d + 1) * shard - q_rows - window + 1) // 16 * 16
        if first < shard:
            pieces.append((d, first))
    kv_rows = sum(shard - first for _, first in pieces)
    cfg = (S, E, lengths.shape[0], cap, RB, F, RP, nc, steps, pieces, tile)
    kvl = keys.shape[1] // HD
    dma = pltpu.SemaphoreType.DMA
    return pl.pallas_call(
        functools.partial(kernel, cfg),
        out_shape=jax.ShapeDtypeStruct((T, S * ff), BF16),
        in_specs=[pl.BlockSpec(memory_space=pl.ANY)] * 7,
        out_specs=pl.BlockSpec(memory_space=pl.ANY),
        scratch_shapes=[
            pltpu.SMEM(lengths.shape, jnp.int32),
            pltpu.VMEM(queries.shape, BF16),
            pltpu.VMEM(keys.shape, BF16),
            pltpu.VMEM(values.shape, BF16),
            pltpu.VMEM((2, T), jnp.int32),
            pltpu.VMEM((2, T), F32),
            pltpu.VMEM((S, T, ff), BF16),
            pltpu.VMEM((E, width, ff), BF16),
            pltpu.VMEM((kv_rows, keys.shape[1]), BF16),
            pltpu.VMEM((kv_rows, keys.shape[1]), BF16),
            pltpu.VMEM((E, 2, T), jnp.int32),
            pltpu.VMEM((E, RB, width), BF16),
            pltpu.VMEM((S, E, RB, width), BF16),
            pltpu.VMEM((RB, ff), F32),
            pltpu.VMEM((E, S, RP, nc), BF16),
            pltpu.VMEM((S, E, RP, nc), BF16),
            dma((6,)),
            dma((E,)),
            dma((2 * len(pieces),)),
            dma((2 * len(pieces),)),
            dma((E,)), dma((E,)), dma((kvl, E)), dma((kvl, E)),
            dma((kvl, E, S)), dma((kvl, E, S)),
            dma((kvl,)),
            dma((len(steps), E, S)), dma((len(steps), E, S)),
            dma((S,)),
        ],
        compiler_params=pltpu.CompilerParams(
            collective_id=0, has_side_effects=True, vmem_limit_bytes=60 * 1024 * 1024
        ),
    )(lengths, queries, keys, values, routes.T, gates.T, w)


def solution(mesh):
    placed = (
        P(("dp", "seq"), "expert"),
        P(("dp", "seq"), "expert"),
        P(("dp", "seq"), "expert"),
        P("dp"),
        P(("dp", "seq", "expert"), None),
        P(("dp", "seq", "expert"), None),
        P("expert", None, "seq"),
    )
    return jax.shard_map(
        shards,
        mesh=mesh,
        in_specs=placed,
        out_specs=P(("dp", "seq", "expert"), None),
        check_vma=False,
    )
```

profile of v0, /device:TPU:0, one launch (start us, length us, event | category | flops | bytes accessed | tf_op | source)
XLA Modules:
  0.0 39.7 jit_solution(6061905114520151197)
XLA Ops:
  0.0 38.0 %shard_map.73 = bf16[16,7168]{1,0:T(8,128)(2,1)} custom-call(s32[8]{0:T(128)} %len_hbm.1, bf16[64,1024]{1,0:T(8,128)(2,1)} %q_hbm.1, bf16[256,256]{1,0:T(8,128)(2,1)} %k_hbm.1, bf16[256,256]{1,0:T(8,128)(2,1)} %v_hbm.1, s32[2,16]{1,0:T(2,128)} %bitcast.4, f32[2,16]{1,0:T(2,128)} %bitcast.5, bf16[4096,3584]{1,0:T(8,128)(2,1)} %bitcast.3), custom_call_target="tpu_custom_call" | custom-call | tf_op jit(solution)/shard_map/pallas_call | solution.py:364
  38.0 1.6 %copy.9 = bf16[16,7168]{1,0:T(8,128)(2,1)} copy(bf16[16,7168]{1,0:T(8,128)(2,1)} %shard_map.73) | data formatting | bytes 458752
where the time goes:
time: 39.8 us; the launch traced here: 39.7 us
  Pallas kernels  38 us (95%)
  local copies, waits for them, and re-layouts  1.64 us (4%)
    pallas_call x1, Pallas kernels, shards(): pl.pallas_call(functools.partial(kernel, cfg), out_shape=jax.ShapeDtypeSt...  38 us
    unnamed x1, local copies, waits for them, and re-layouts  1.64 us

commit v1 on v0

v1 whole, which is shorter than its diff:
```python
import functools

import jax
import jax.numpy as jnp
from jax import lax
from jax.experimental import pallas as pl
from jax.experimental.pallas import tpu as pltpu
from jax.sharding import PartitionSpec as P

HD = 128
MESH = pl.DeviceIdType.MESH
F32 = jnp.float32
BF16 = jnp.bfloat16
NT = (((1,), (1,)), ((), ()))


def up(n, m):
    return -(-n // m) * m


def iota(shape, dim):
    return lax.broadcasted_iota(jnp.int32, shape, dim)


def onehot(mask):
    return jnp.where(mask, F32(1.0), F32(0.0)).astype(BF16)


def dot(a, b):
    return jnp.dot(a, b, preferred_element_type=F32)


def kernel(
    cfg,
    len_hbm, q_hbm, k_hbm, v_hbm, routes_hbm, gates_hbm, w_hbm, out_ref,
    len_ref, q_ref, k_ref, v_ref, routes_ref, gates_ref,
    wbuf, kvbuf, rbuf, xbuf, acc, sendbuf, recv,
    in_sem, w_sem, kv_send, kv_recv, r_send, r_recv, z_send, z_recv, x_send, x_recv,
    b_send, b_recv,
):
    S, E, ndoc, cap, F, RP, nc, steps, pieces, tile = cfg
    s = lax.axis_index("seq")
    e = lax.axis_index("expert")
    Q, width = q_ref.shape
    shard = k_ref.shape[0]
    kvl = k_ref.shape[1] // HD
    group = width // HD // kvl
    hw = group * HD
    T = routes_ref.shape[1]
    ff = w_hbm.shape[1]
    depth = w_hbm.shape[0]
    scale = 1.0 / HD**0.5

    def at_s(d):
        return lax.rem(s + S - d, S)

    def at_e(d):
        return lax.rem(e + E - d, E)

    barrier = pltpu.get_barrier_semaphore()
    for ds in range(S):
        for de in range(E):
            if ds or de:
                pl.semaphore_signal(
                    barrier, inc=1, device_id={"seq": at_s(ds), "expert": at_e(de)},
                    device_id_type=MESH,
                )

    near = [sorted(range(E), key=lambda o, n=n: (abs(o - n), o)) for n in range(E)]
    origin = [e]
    for k in range(1, E):
        o = near[0][k]
        for n in range(1, E):
            o = jnp.where(e == n, near[n][k], o)
        origin.append(o)

    def w_copy(k):
        return pltpu.make_async_copy(
            w_hbm.at[pl.ds(pl.multiple_of(origin[k] * width, width), width)],
            wbuf.at[origin[k]], w_sem.at[k],
        )

    ins = []
    for i, (src, dst) in enumerate((
        (k_hbm, k_ref), (q_hbm, q_ref), (v_hbm, v_ref), (len_hbm, len_ref),
        (routes_hbm, routes_ref), (gates_hbm, gates_ref),
    )):
        c = pltpu.make_async_copy(src, dst, in_sem.at[i])
        c.start()
        ins.append(c)
    for c in ins[:5]:
        c.wait()

    def remote(src, dst, ssem, rsem, to_s, to_e):
        return pltpu.make_async_remote_copy(
            src_ref=src, dst_ref=dst, send_sem=ssem, recv_sem=rsem,
            device_id={"seq": to_s, "expert": to_e}, device_id_type=MESH,
        )

    def all_of(ref, sem):
        return pltpu.make_async_copy(ref, ref, sem)

    for k in range(E):
        w_copy(k).start()

    qn = group * Q
    qpos = s * shard + shard - Q + lax.rem(iota((qn, 1), 0), Q)
    docstart = jnp.zeros((qn, 1), jnp.int32)
    begin = jnp.int32(0)
    for j in range(ndoc):
        docstart = jnp.where(qpos >= begin, begin, docstart)
        begin = begin + len_ref[j]

    def masked(q, k, first):
        sc = lax.dot_general(q, k, NT, preferred_element_type=F32) * scale
        kpos = first + iota((1, k.shape[0]), 1)
        return jnp.where((kpos <= qpos) & (kpos >= docstart), sc, F32(-1e30))

    queries = []
    local = []
    for h in range(kvl):
        q = jnp.concatenate(
            [q_ref[:, (h * group + g) * HD:(h * group + g + 1) * HD] for g in range(group)], axis=0
        )
        queries.append(q)
        sc = masked(q, k_ref[:, h * HD:(h + 1) * HD], s * shard)
        peak = jnp.max(sc, axis=-1, keepdims=True)
        wt = jnp.exp(sc - peak)
        local.append((peak, jnp.sum(wt, axis=-1, keepdims=True),
                      dot(wt.astype(BF16), v_ref[:, h * HD:(h + 1) * HD])))

    pl.semaphore_wait(barrier, S * E - 1)

    spans = []
    offset = 0
    for d, first in pieces:
        spans.append((offset, shard - first))
        offset += shard - first
    for h in range(kvl):
        for i, (d, first) in enumerate(pieces):
            @pl.when(s + d < S)
            def _():
                lo, n = spans[i]
                for j, ref in enumerate((k_ref, v_ref)):
                    remote(
                        ref.at[pl.ds(first, n), pl.ds(h * HD, HD)],
                        kvbuf.at[h, j, pl.ds(lo, n)],
                        kv_send.at[i], kv_recv.at[i, h], s + d, e,
                    ).start()
    for ds in range(S):
        for de in range(E):
            if ds or de:
                remote(routes_ref, rbuf.at[ds * E + de], r_send.at[0], r_recv.at[0],
                       at_s(ds), at_e(de)).start()

    def part(h):
        return pl.ds(h * hw, hw)

    def spread(o, h, rising, falling):
        src = xbuf.at[0, o, :, part(h)]

        @pl.when(rising)
        def _():
            remote(src, src, z_send.at[0], z_recv.at[o, h], s, e + 1).start()

        @pl.when(falling)
        def _():
            remote(src, src, z_send.at[1], z_recv.at[o, h], s, e - 1).start()

        for ds in range(1, S):
            remote(src, xbuf.at[ds, o, :, part(h)], x_send.at[0], x_recv.at[ds - 1, o, h],
                   at_s(ds), e).start()

    def store_head(h, got, total):
        att = (got / total).astype(BF16)
        for g in range(group):
            cols = slice((h * group + g) * HD, (h * group + g + 1) * HD)
            xbuf[0, e, :, cols] = att[g * Q:(g + 1) * Q]

    for h in range(kvl):
        peak, total, got = local[h]

        @pl.when(s == 0)
        def _():
            store_head(h, got, total)

        @pl.when(s > 0)
        def _():
            q = queries[h]
            run_peak, run_total, run_got = peak, total, got
            for i, (d, first) in enumerate(pieces):
                lo, n = spans[i]
                if d > 1:
                    @pl.when(s < d)
                    def _():
                        kvbuf[h, :, lo:lo + n] = jnp.zeros((2, n, HD), BF16)

                @pl.when(s >= d)
                def _():
                    all_of(kvbuf.at[h, :, pl.ds(lo, n)], kv_recv.at[i, h]).wait()

                sc = masked(q, kvbuf[h, 0, lo:lo + n], (s - d) * shard + first)
                higher = jnp.maximum(run_peak, jnp.max(sc, axis=-1, keepdims=True))
                wt = jnp.exp(sc - higher)
                fade = jnp.exp(run_peak - higher)
                run_total = run_total * fade + jnp.sum(wt, axis=-1, keepdims=True)
                run_got = run_got * fade + dot(wt.astype(BF16), kvbuf[h, 1, lo:lo + n])
                run_peak = higher
            store_head(h, run_got, run_total)

        spread(e, h, e + 1 < E, e > 0)

    def squares(g, o):
        xf = xbuf[g, o].astype(F32)
        return jnp.sum(xf * xf, axis=-1, keepdims=True)

    w_copy(0).wait()
    square = squares(0, e)
    x = xbuf[0, e]
    for c0 in range(0, ff, tile):
        acc[:, c0:c0 + tile] = dot(x, wbuf[e, :, c0:c0 + tile])

    all_of(rbuf.at[pl.ds(1, S * E - 1)], r_recv.at[0]).wait()
    mine = routes_ref[...]
    names = iota((up(E, 8), 1), 0)
    upper = onehot(iota((T, T), 0) < iota((T, T), 1))

    def ranks(rt):
        mt = onehot((rt[0:1, :] == names) | (rt[1:2, :] == names))
        return mt, dot(mt, upper)

    rows_out, rows_in = E * RP, F * Q
    out_row = iota((rows_out, 1), 0)
    in_row = iota((1, rows_in), 1)
    inner = lax.rem(out_row, RP)
    to_block = lax.rem(e + E - lax.div(out_row, RP), E)
    fold = jnp.where(inner < F * cap, lax.div(inner, cap), F)
    slot = (lax.rem(inner, cap) + 1).astype(F32)
    same = (fold == lax.div(in_row, Q)) & (to_block == lax.div(lax.rem(in_row, Q), T))
    own_before = None
    perms = []
    for g in range(S):
        placed = jnp.zeros((up(E, 8), rows_in), F32)
        for de in range(E):
            mt, cnt = ranks(mine if g == 0 and de == 0 else rbuf[g * E + de])
            if own_before is None:
                own_before = cnt
            place = jnp.where(mt > 0.5, cnt + 1.0, F32(0.0)).astype(BF16)
            shift = onehot(iota((T, rows_in), 0) + lax.rem(e + de, E) * T
                           == lax.rem(iota((T, rows_in), 1), Q))
            placed = placed + dot(place, shift)
        row = jnp.sum(jnp.where(names == e, placed, F32(0.0)), axis=0, keepdims=True)
        perms.append(onehot(same & (row == slot)))

    sends = []

    def give_back(g, square, product):
        factor = lax.rsqrt(square / depth + 1e-05)
        to = at_s(S - g) if g else s
        half = (S - g) % S
        for st, (c0, n) in enumerate(steps):
            folded = []
            for f in range(F):
                part = product(slice(f * nc + c0, f * nc + c0 + n)) * factor
                folded.append((part / (1.0 + jnp.exp(-part))).astype(BF16))
            moved = dot(perms[g], jnp.concatenate(folded, axis=0)).astype(BF16)
            for de in range(E):
                block = moved[de * RP:(de + 1) * RP]
                if g or de:
                    sendbuf[g * E + de, :, c0:c0 + n] = block
                else:
                    recv[0, 0, :, c0:c0 + n] = block
            for de in reversed(range(E)):
                if g or de:
                    c = remote(sendbuf.at[g * E + de, :, pl.ds(c0, n)],
                               recv.at[half, de, :, pl.ds(c0, n)],
                               b_send.at[0], b_recv.at[half, st], to, at_e(de))
                    c.start()

    for k in range(1, E):
        o = origin[k]
        for h in range(kvl):
            all_of(xbuf.at[0, o, :, part(h)], z_recv.at[o, h]).wait()
            spread(o, h, (o < e) & (e + 1 < E), (o > e) & (e > 0))
        w_copy(k).wait()
        square = square + squares(0, o)
        x = xbuf[0, o]
        if k < E - 1:
            for c0 in range(0, ff, tile):
                acc[:, c0:c0 + tile] += dot(x, wbuf[o, :, c0:c0 + tile])
        else:
            give_back(0, square, lambda cols: acc[:, cols] + dot(x, wbuf[o, :, cols]))

    for g in range(1, S):
        square = jnp.zeros((Q, 1), F32)
        for o in range(E):
            for h in range(kvl):
                all_of(xbuf.at[g, o, :, part(h)], x_recv.at[g - 1, o, h]).wait()
            square = square + squares(g, o)

        def whole(cols, g=g):
            total = dot(xbuf[g, 0], wbuf[0, :, cols])
            for o in range(1, E):
                total = total + dot(xbuf[g, o], wbuf[o, :, cols])
            return total

        give_back(g, square, whole)

    ins[5].wait()
    diagonal = iota((T, T), 0) == iota((T, T), 1)

    def column(row):
        return jnp.sum(jnp.where(diagonal, row, jnp.zeros_like(row)), axis=1, keepdims=True)

    wide = iota((T, E * RP), 1)
    at = []
    for k in range(2):
        rk = mine[k:k + 1, :]
        rank = jnp.sum(jnp.where(rk == names, own_before, F32(0.0)), axis=0, keepdims=True)
        rel = rk - e
        rel = jnp.where(rel < 0, rel + E, rel)
        at.append(column((rel * RP).astype(F32) + rank).astype(jnp.int32))
    pick = jnp.concatenate(
        [onehot(at[k] + f * cap == wide) for f in range(F) for k in range(2)], axis=0
    )
    g0, g1 = column(gates_ref[0:1, :]), column(gates_ref[1:2, :])

    for half in range(S):
        base = lax.rem(s + half, S) * ff
        for st, (c0, n) in enumerate(steps):
            came = recv.at[half, pl.ds(0 if half else 1, E if half else E - 1), :, pl.ds(c0, n)]
            all_of(came, b_recv.at[half, st]).wait()
            got = recv[half, :, :, c0:c0 + n].reshape(E * RP, n)
            res = dot(pick, got)
            for f in range(F):
                lo = 2 * f * T
                mix = g0 * res[lo:lo + T] + g1 * res[lo + T:lo + 2 * T]
                cols = pl.ds(pl.multiple_of(base + f * nc + c0, 128), n)
                out_ref[:, cols] = mix.astype(BF16)

    for i, (d, first) in enumerate(pieces):
        @pl.when(s + d < S)
        def _():
            lo, n = spans[i]
            all_of(kvbuf.at[:, :, pl.ds(lo, n)], kv_send.at[i]).wait()
    all_of(rbuf.at[pl.ds(1, S * E - 1)], r_send.at[0]).wait()
    for n in range(E):
        @pl.when(e == n)
        def _():
            if n + 1 < E:
                all_of(xbuf.at[0, pl.ds(0, n + 1)], z_send.at[0]).wait()
            if n > 0:
                all_of(xbuf.at[0, pl.ds(0, E - n)], z_send.at[1]).wait()
    all_of(xbuf.at[pl.ds(0, S - 1)], x_send.at[0]).wait()
    all_of(sendbuf.at[pl.ds(0, S * E - 1)], b_send.at[0]).wait()


def shards(queries, keys, values, lengths, routes, gates, w_up):
    S, E = lax.axis_size("seq"), lax.axis_size("expert")
    q_rows, width = queries.shape
    shard = keys.shape[0]
    w = w_up.reshape(w_up.shape[1], w_up.shape[2])
    depth, ff = w.shape
    T = routes.shape[0]
    cap = max(2, 3 * q_rows // (E * E))
    choices = [f for f in range(1, ff // 128 + 1) if ff % (f * 128) == 0]
    F = min(choices, key=lambda f: up(f * cap, 16) * (ff // f))
    RP = up(F * cap, 16)
    nc = ff // F
    cuts = list(range(0, max(nc - 255, 1), 256))
    steps = [(c, (cuts + [nc])[i + 1] - c) for i, c in enumerate(cuts)]
    tile = 512 if ff % 512 == 0 else 128
    window = shard * S // 2
    pieces = []
    for d in range(1, S):
        first = max(0, (d + 1) * shard - q_rows - window + 1) // 16 * 16
        if first < shard:
            pieces.append((d, first))
    kv_rows = sum(shard - first for _, first in pieces)
    cfg = (S, E, lengths.shape[0], cap, F, RP, nc, steps, pieces, tile)
    kvl = keys.shape[1] // HD
    dma = pltpu.SemaphoreType.DMA
    args = [
        pltpu.with_memory_space_constraint(a, pltpu.HBM)
        for a in (lengths, queries, keys, values, routes.T, gates.T, w)
    ]
    return pl.pallas_call(
        functools.partial(kernel, cfg),
        out_shape=pltpu.VMEM((T, S * ff), BF16),
        in_specs=[pl.BlockSpec(memory_space=pltpu.HBM)] * 7,
        out_specs=pl.BlockSpec(memory_space=pltpu.VMEM),
        scratch_shapes=[
            pltpu.SMEM(lengths.shape, jnp.int32),
            pltpu.VMEM(queries.shape, BF16),
            pltpu.VMEM(keys.shape, BF16),
            pltpu.VMEM(values.shape, BF16),
            pltpu.VMEM((2, T), jnp.int32),
            pltpu.VMEM((2, T), F32),
            pltpu.VMEM((E, width, ff), BF16),
            pltpu.VMEM((kvl, 2, kv_rows, HD), BF16),
            pltpu.VMEM((S * E, 2, T), jnp.int32),
            pltpu.VMEM((S, E, q_rows, width), BF16),
            pltpu.VMEM((q_rows, ff), F32),
            pltpu.VMEM((S * E, RP, nc), BF16),
            pltpu.VMEM((S, E, RP, nc), BF16),
            dma((6,)),
            dma((E,)),
            dma((len(pieces),)),
            dma((len(pieces), kvl)),
            dma((1,)), dma((1,)),
            dma((2,)), dma((E, kvl)),
            dma((1,)), dma((S - 1, E, kvl)),
            dma((1,)), dma((S, len(steps))),
        ],
        compiler_params=pltpu.CompilerParams(
            collective_id=0, has_side_effects=True, vmem_limit_bytes=60 * 1024 * 1024
        ),
    )(*args)


def solution(mesh):
    placed = (
        P(("dp", "seq"), "expert"),
        P(("dp", "seq"), "expert"),
        P(("dp", "seq"), "expert"),
        P("dp"),
        P(("dp", "seq", "expert"), None),
        P(("dp", "seq", "expert"), None),
        P("expert", None, "seq"),
    )
    return jax.shard_map(
        shards,
        mesh=mesh,
        in_specs=placed,
        out_specs=P(("dp", "seq", "expert"), None),
        check_vma=False,
    )
```

time: 39.8 us -> 41 us (1.030)
  Pallas kernels: 38 us -> 40.1 us
  local copies, waits for them, and re-layouts: 1.64 us -> 0.69 us
    pallas_call x1, Pallas kernels: 38 us -> 40.1 us  [shards(): pl.pallas_call(functools.partial(kernel, cfg), out_shape=pltpu.VMEM((T, S...]
    unnamed x1, local copies, waits for them, and re-layouts: 1.64 us -> 0.69 us
where the time goes in v1:
time: 41 us; the launch traced here: 40.8 us
  Pallas kernels  40.1 us (98%)
  local copies, waits for them, and re-layouts  0.69 us (2%)
    pallas_call x1, Pallas kernels, shards(): pl.pallas_call(functools.partial(kernel, cfg), out_shape=pltpu.VMEM((T, S...  40.1 us

profile of v1, /device:TPU:0, one launch (start us, length us, event | category | flops | bytes accessed | tf_op | source)
XLA Modules:
  0.0 40.8 jit_solution(6631815459384860755)
XLA Ops:
  0.0 40.1 %shard_map.73 = bf16[16,7168]{1,0:T(8,128)(2,1)S(1)} custom-call(s32[8]{0:T(128)} %len_hbm.1, bf16[64,1024]{1,0:T(8,128)(2,1)} %q_hbm.1, bf16[256,256]{1,0:T(8,128)(2,1)} %k_hbm.1, bf16[256,256]{1,0:T(8,128)(2,1)} %v_hbm.1, s32[2,16]{1,0:T(2,128)} %bitcast.4, f32[2,16]{1,0:T(2,128)} %bitcast.5, bf16[4096,3584]{1,0:T(8,128)(2,1)} %bitcast.3), custom_call_target="tpu_custom_call" | custom-call | tf_op jit(solution)/shard_map/pallas_call | solution.py:387
  40.1 0.7 %copy.9 = bf16[16,7168]{1,0:T(8,128)(2,1)} copy(bf16[16,7168]{1,0:T(8,128)(2,1)S(1)} %shard_map.73) | data formatting | bytes 458752

commit v2 on v1

--- a/solution.py
+++ b/solution.py
@@ -34,11 +34,11 @@
     cfg,
     len_hbm, q_hbm, k_hbm, v_hbm, routes_hbm, gates_hbm, w_hbm, out_ref,
     len_ref, q_ref, k_ref, v_ref, routes_ref, gates_ref,
-    wbuf, kvbuf, rbuf, xbuf, acc, sendbuf, recv,
+    wbuf, kvbuf, rbuf, pack, xbuf, acc, sendbuf, recv,
     in_sem, w_sem, kv_send, kv_recv, r_send, r_recv, z_send, z_recv, x_send, x_recv,
     b_send, b_recv,
 ):
-    S, E, ndoc, cap, F, RP, nc, steps, pieces, tile = cfg
+    S, E, ndoc, cap, RB, F, RP, nc, steps, pieces, tile = cfg
     s = lax.axis_index("seq")
     e = lax.axis_index("expert")
     Q, width = q_ref.shape
@@ -147,35 +147,44 @@
                         kvbuf.at[h, j, pl.ds(lo, n)],
                         kv_send.at[i], kv_recv.at[i, h], s + d, e,
                     ).start()
-    for ds in range(S):
-        for de in range(E):
-            if ds or de:
-                remote(routes_ref, rbuf.at[ds * E + de], r_send.at[0], r_recv.at[0],
-                       at_s(ds), at_e(de)).start()
+    for de in range(1, E):
+        remote(routes_ref, rbuf.at[de], r_send.at[0], r_recv.at[0], s, at_e(de)).start()
 
     def part(h):
         return pl.ds(h * hw, hw)
 
-    def spread(o, h, rising, falling):
-        src = xbuf.at[0, o, :, part(h)]
-
-        @pl.when(rising)
-        def _():
-            remote(src, src, z_send.at[0], z_recv.at[o, h], s, e + 1).start()
-
-        @pl.when(falling)
-        def _():
-            remote(src, src, z_send.at[1], z_recv.at[o, h], s, e - 1).start()
-
+    def relay(src, o, h):
         for ds in range(1, S):
             remote(src, xbuf.at[ds, o, :, part(h)], x_send.at[0], x_recv.at[ds - 1, o, h],
                    at_s(ds), e).start()
+
+    all_of(rbuf.at[pl.ds(1, E - 1)], r_recv.at[0]).wait()
+    mine = routes_ref[...]
+    names = iota((up(E, 8), 1), 0)
+    upper = onehot(iota((T, T), 0) < iota((T, T), 1))
+    total_place = jnp.zeros((up(E, 8), Q), F32)
+    for de in range(E):
+        rt = mine if de == 0 else rbuf[de]
+        mt = onehot((rt[0:1, :] == names) | (rt[1:2, :] == names))
+        cnt = dot(mt, upper)
+        blk = lax.rem(e + de, E)
+        place = jnp.where(mt > 0.5, cnt + (blk * cap).astype(F32) + 1.0, F32(0.0))
+        if de == 0:
+            before = cnt
+        shift = onehot(iota((T, Q), 0) + blk * T == iota((T, Q), 1))
+        total_place = total_place + dot(place.astype(BF16), shift)
+    row_of = iota((RB, Q), 0).astype(F32) + 1.0
+    selector = jnp.concatenate(
+        [onehot(total_place[x:x + 1, :] == row_of) for x in range(E)], axis=0
+    )
 
     def store_head(h, got, total):
         att = (got / total).astype(BF16)
         for g in range(group):
             cols = slice((h * group + g) * HD, (h * group + g + 1) * HD)
-            xbuf[0, e, :, cols] = att[g * Q:(g + 1) * Q]
+            packed = dot(selector, att[g * Q:(g + 1) * Q]).astype(BF16)
+            for x in range(E):
+                pack[x, :, cols] = packed[x * RB:(x + 1) * RB]
 
     for h in range(kvl):
         peak, total, got = local[h]
@@ -208,51 +217,31 @@
                 run_peak = higher
             store_head(h, run_got, run_total)
 
-        spread(e, h, e + 1 < E, e > 0)
+        for k in range(1, E):
+            to = origin[k]
+            remote(pack.at[to, :, part(h)], xbuf.at[0, e, :, part(h)],
+                   z_send.at[0], z_recv.at[e, h], s, to).start()
+        relay(pack.at[e, :, part(h)], e, h)
+
 
     def squares(g, o):
         xf = xbuf[g, o].astype(F32)
         return jnp.sum(xf * xf, axis=-1, keepdims=True)
 
     w_copy(0).wait()
+    xbuf[0, e] = pack[e]
     square = squares(0, e)
     x = xbuf[0, e]
     for c0 in range(0, ff, tile):
         acc[:, c0:c0 + tile] = dot(x, wbuf[e, :, c0:c0 + tile])
 
-    all_of(rbuf.at[pl.ds(1, S * E - 1)], r_recv.at[0]).wait()
-    mine = routes_ref[...]
-    names = iota((up(E, 8), 1), 0)
-    upper = onehot(iota((T, T), 0) < iota((T, T), 1))
-
-    def ranks(rt):
-        mt = onehot((rt[0:1, :] == names) | (rt[1:2, :] == names))
-        return mt, dot(mt, upper)
-
-    rows_out, rows_in = E * RP, F * Q
+    rows_out, rows_in = E * RP, F * RB
     out_row = iota((rows_out, 1), 0)
-    in_row = iota((1, rows_in), 1)
     inner = lax.rem(out_row, RP)
-    to_block = lax.rem(e + E - lax.div(out_row, RP), E)
-    fold = jnp.where(inner < F * cap, lax.div(inner, cap), F)
-    slot = (lax.rem(inner, cap) + 1).astype(F32)
-    same = (fold == lax.div(in_row, Q)) & (to_block == lax.div(lax.rem(in_row, Q), T))
-    own_before = None
-    perms = []
-    for g in range(S):
-        placed = jnp.zeros((up(E, 8), rows_in), F32)
-        for de in range(E):
-            mt, cnt = ranks(mine if g == 0 and de == 0 else rbuf[g * E + de])
-            if own_before is None:
-                own_before = cnt
-            place = jnp.where(mt > 0.5, cnt + 1.0, F32(0.0)).astype(BF16)
-            shift = onehot(iota((T, rows_in), 0) + lax.rem(e + de, E) * T
-                           == lax.rem(iota((T, rows_in), 1), Q))
-            placed = placed + dot(place, shift)
-        row = jnp.sum(jnp.where(names == e, placed, F32(0.0)), axis=0, keepdims=True)
-        perms.append(onehot(same & (row == slot)))
-
-    sends = []
+    e_of = lax.rem(e + E - lax.div(out_row, RP), E)
+    from_row = lax.div(inner, cap) * RB + e_of * cap + lax.rem(inner, cap)
+    from_row = jnp.where(inner < F * cap, from_row, -1)
+    perm = onehot(from_row == iota((rows_out, rows_in), 1))
 
     def give_back(g, square, product):
         factor = lax.rsqrt(square / depth + 1e-05)
@@ -263,7 +252,7 @@
             for f in range(F):
                 part = product(slice(f * nc + c0, f * nc + c0 + n)) * factor
                 folded.append((part / (1.0 + jnp.exp(-part))).astype(BF16))
-            moved = dot(perms[g], jnp.concatenate(folded, axis=0)).astype(BF16)
+            moved = dot(perm, jnp.concatenate(folded, axis=0)).astype(BF16)
             for de in range(E):
                 block = moved[de * RP:(de + 1) * RP]
                 if g or de:
@@ -281,7 +270,7 @@
         o = origin[k]
         for h in range(kvl):
             all_of(xbuf.at[0, o, :, part(h)], z_recv.at[o, h]).wait()
-            spread(o, h, (o < e) & (e + 1 < E), (o > e) & (e > 0))
+            relay(xbuf.at[0, o, :, part(h)], o, h)
         w_copy(k).wait()
         square = square + squares(0, o)
         x = xbuf[0, o]
@@ -292,7 +281,7 @@
             give_back(0, square, lambda cols: acc[:, cols] + dot(x, wbuf[o, :, cols]))
 
     for g in range(1, S):
-        square = jnp.zeros((Q, 1), F32)
+        square = jnp.zeros((RB, 1), F32)
         for o in range(E):
             for h in range(kvl):
                 all_of(xbuf.at[g, o, :, part(h)], x_recv.at[g - 1, o, h]).wait()
@@ -316,7 +305,7 @@
     at = []
     for k in range(2):
         rk = mine[k:k + 1, :]
-        rank = jnp.sum(jnp.where(rk == names, own_before, F32(0.0)), axis=0, keepdims=True)
+        rank = jnp.sum(jnp.where(rk == names, before, F32(0.0)), axis=0, keepdims=True)
         rel = rk - e
         rel = jnp.where(rel < 0, rel + E, rel)
         at.append(column((rel * RP).astype(F32) + rank).astype(jnp.int32))
@@ -343,14 +332,8 @@
         def _():
             lo, n = spans[i]
             all_of(kvbuf.at[:, :, pl.ds(lo, n)], kv_send.at[i]).wait()
-    all_of(rbuf.at[pl.ds(1, S * E - 1)], r_send.at[0]).wait()
-    for n in range(E):
-        @pl.when(e == n)
-        def _():
-            if n + 1 < E:
-                all_of(xbuf.at[0, pl.ds(0, n + 1)], z_send.at[0]).wait()
-            if n > 0:
-                all_of(xbuf.at[0, pl.ds(0, E - n)], z_send.at[1]).wait()
+    all_of(rbuf.at[pl.ds(1, E - 1)], r_send.at[0]).wait()
+    all_of(pack.at[pl.ds(0, E - 1)], z_send.at[0]).wait()
     all_of(xbuf.at[pl.ds(0, S - 1)], x_send.at[0]).wait()
     all_of(sendbuf.at[pl.ds(0, S * E - 1)], b_send.at[0]).wait()
 
@@ -364,6 +347,7 @@
     T = routes.shape[0]
     cap = max(2, 3 * q_rows // (E * E))
     choices = [f for f in range(1, ff // 128 + 1) if ff % (f * 128) == 0]
+    RB = up(E * cap, 16)
     F = min(choices, key=lambda f: up(f * cap, 16) * (ff // f))
     RP = up(F * cap, 16)
     nc = ff // F
@@ -377,7 +361,7 @@
         if first < shard:
             pieces.append((d, first))
     kv_rows = sum(shard - first for _, first in pieces)
-    cfg = (S, E, lengths.shape[0], cap, F, RP, nc, steps, pieces, tile)
+    cfg = (S, E, lengths.shape[0], cap, RB, F, RP, nc, steps, pieces, tile)
     kvl = keys.shape[1] // HD
     dma = pltpu.SemaphoreType.DMA
     args = [
@@ -398,9 +382,10 @@
             pltpu.VMEM((2, T), F32),
             pltpu.VMEM((E, width, ff), BF16),
             pltpu.VMEM((kvl, 2, kv_rows, HD), BF16),
-            pltpu.VMEM((S * E, 2, T), jnp.int32),
-            pltpu.VMEM((S, E, q_rows, width), BF16),
-            pltpu.VMEM((q_rows, ff), F32),
+            pltpu.VMEM((E, 2, T), jnp.int32),
+            pltpu.VMEM((E, RB, width), BF16),
+            pltpu.VMEM((S, E, RB, width), BF16),
+            pltpu.VMEM((RB, ff), F32),
             pltpu.VMEM((S * E, RP, nc), BF16),
             pltpu.VMEM((S, E, RP, nc), BF16),
             dma((6,)),
@@ -408,7 +393,7 @@
             dma((len(pieces),)),
             dma((len(pieces), kvl)),
             dma((1,)), dma((1,)),
-            dma((2,)), dma((E, kvl)),
+            dma((1,)), dma((E, kvl)),
             dma((1,)), dma((S - 1, E, kvl)),
             dma((1,)), dma((S, len(steps))),
         ],

time: 41 us -> 36.1 us (0.88)
  Pallas kernels: 40.1 us -> 35.2 us
    pallas_call x1, Pallas kernels: 40.1 us -> 35.2 us  [shards(): pl.pallas_call(functools.partial(kernel, cfg), out_shape=pltpu.VMEM((T, S...]
where the time goes in v2:
time: 36.1 us; the launch traced here: 35.9 us
  Pallas kernels  35.2 us (98%)
  local copies, waits for them, and re-layouts  0.69 us (2%)
    pallas_call x1, Pallas kernels, shards(): pl.pallas_call(functools.partial(kernel, cfg), out_shape=pltpu.VMEM((T, S...  35.2 us

profile of v2, /device:TPU:0, one launch (start us, length us, event | category | flops | bytes accessed | tf_op | source)
XLA Modules:
  0.0 35.9 jit_solution(14361856284671544905)
XLA Ops:
  0.0 35.2 %shard_map.73 = bf16[16,7168]{1,0:T(8,128)(2,1)S(1)} custom-call(s32[8]{0:T(128)} %len_hbm.1, bf16[64,1024]{1,0:T(8,128)(2,1)} %q_hbm.1, bf16[256,256]{1,0:T(8,128)(2,1)} %k_hbm.1, bf16[256,256]{1,0:T(8,128)(2,1)} %v_hbm.1, s32[2,16]{1,0:T(2,128)} %bitcast.4, f32[2,16]{1,0:T(2,128)} %bitcast.5, bf16[4096,3584]{1,0:T(8,128)(2,1)} %bitcast.3), custom_call_target="tpu_custom_call" | custom-call | tf_op jit(solution)/shard_map/pallas_call | solution.py:371
  35.2 0.7 %copy.9 = bf16[16,7168]{1,0:T(8,128)(2,1)} copy(bf16[16,7168]{1,0:T(8,128)(2,1)S(1)} %shard_map.73) | data formatting | bytes 458752

commit v3 on v2

--- a/solution.py
+++ b/solution.py
@@ -34,9 +34,9 @@
     cfg,
     len_hbm, q_hbm, k_hbm, v_hbm, routes_hbm, gates_hbm, w_hbm, out_ref,
     len_ref, q_ref, k_ref, v_ref, routes_ref, gates_ref,
-    wbuf, kvbuf, rbuf, pack, xbuf, acc, sendbuf, recv,
+    wbuf, kvbuf, rbuf, raw, nbuf, fwd, sel_ref, pack, xbuf, acc, square_ref, sendbuf, recv,
     in_sem, w_sem, kv_send, kv_recv, r_send, r_recv, z_send, z_recv, x_send, x_recv,
-    b_send, b_recv,
+    b_send, b_recv, n_recv,
 ):
     S, E, ndoc, cap, RB, F, RP, nc, steps, pieces, tile = cfg
     s = lax.axis_index("seq")
@@ -60,19 +60,28 @@
     barrier = pltpu.get_barrier_semaphore()
     for ds in range(S):
         for de in range(E):
-            if ds or de:
+            if (ds == 0) != (de == 0):
                 pl.semaphore_signal(
                     barrier, inc=1, device_id={"seq": at_s(ds), "expert": at_e(de)},
                     device_id_type=MESH,
                 )
 
-    near = [sorted(range(E), key=lambda o, n=n: (abs(o - n), o)) for n in range(E)]
+    mid = (E // 2 - 1, E // 2)
+
+    def key(n, o):
+        return (o != n, not (n in mid and o in mid), abs(o - n), o)
+
+    near = [sorted(range(E), key=functools.partial(key, n)) for n in range(E)]
     origin = [e]
     for k in range(1, E):
         o = near[0][k]
         for n in range(1, E):
             o = jnp.where(e == n, near[n][k], o)
         origin.append(o)
+
+    inner_dev = (e == mid[0]) | (e == mid[1])
+    side = lax.div(e, E // 2)
+    across = E - 1 - e
 
     def w_copy(k):
         return pltpu.make_async_copy(
@@ -129,7 +138,7 @@
         local.append((peak, jnp.sum(wt, axis=-1, keepdims=True),
                       dot(wt.astype(BF16), v_ref[:, h * HD:(h + 1) * HD])))
 
-    pl.semaphore_wait(barrier, S * E - 1)
+    pl.semaphore_wait(barrier, S + E - 2)
 
     spans = []
     offset = 0
@@ -158,6 +167,22 @@
             remote(src, xbuf.at[ds, o, :, part(h)], x_send.at[0], x_recv.at[ds - 1, o, h],
                    at_s(ds), e).start()
 
+    def store_head(h, got, total):
+        att = (got / total).astype(BF16)
+        for g in range(group):
+            cols = slice((h * group + g) * HD, (h * group + g + 1) * HD)
+            raw[:, cols] = att[g * Q:(g + 1) * Q]
+
+        @pl.when(inner_dev)
+        def _():
+            remote(raw.at[:, part(h)], nbuf.at[:, part(h)], z_send.at[1], n_recv.at[h],
+                   s, across).start()
+
+    @pl.when(s == 0)
+    def _():
+        for h in range(kvl):
+            store_head(h, local[h][2], local[h][1])
+
     all_of(rbuf.at[pl.ds(1, E - 1)], r_recv.at[0]).wait()
     mine = routes_ref[...]
     names = iota((up(E, 8), 1), 0)
@@ -174,24 +199,21 @@
         shift = onehot(iota((T, Q), 0) + blk * T == iota((T, Q), 1))
         total_place = total_place + dot(place.astype(BF16), shift)
     row_of = iota((RB, Q), 0).astype(F32) + 1.0
-    selector = jnp.concatenate(
-        [onehot(total_place[x:x + 1, :] == row_of) for x in range(E)], axis=0
-    )
-
-    def store_head(h, got, total):
-        att = (got / total).astype(BF16)
-        for g in range(group):
-            cols = slice((h * group + g) * HD, (h * group + g + 1) * HD)
-            packed = dot(selector, att[g * Q:(g + 1) * Q]).astype(BF16)
-            for x in range(E):
-                pack[x, :, cols] = packed[x * RB:(x + 1) * RB]
+    chosen = [onehot(total_place[x:x + 1, :] == row_of) for x in range(E)]
+    selector = jnp.concatenate(chosen, axis=0)
+    for x in range(E):
+        sel_ref[x] = chosen[x]
+
+    def send(k, h):
+        to = origin[k]
+
+        @pl.when(jnp.logical_not(inner_dev) | (lax.div(to, E // 2) == side))
+        def _():
+            remote(pack.at[to, :, part(h)], xbuf.at[0, e, :, part(h)],
+                   z_send.at[0], z_recv.at[e, h], s, to).start()
 
     for h in range(kvl):
         peak, total, got = local[h]
-
-        @pl.when(s == 0)
-        def _():
-            store_head(h, got, total)
 
         @pl.when(s > 0)
         def _():
@@ -217,23 +239,63 @@
                 run_peak = higher
             store_head(h, run_got, run_total)
 
-        for k in range(1, E):
-            to = origin[k]
-            remote(pack.at[to, :, part(h)], xbuf.at[0, e, :, part(h)],
-                   z_send.at[0], z_recv.at[e, h], s, to).start()
+        packed = dot(selector, raw[:, h * hw:(h + 1) * hw]).astype(BF16)
+        for x in range(E):
+            pack[x, :, h * hw:(h + 1) * hw] = packed[x * RB:(x + 1) * RB]
+        if h == 0:
+            for k in range(1, E - 1):
+                send(k, h)
         relay(pack.at[e, :, part(h)], e, h)
-
+    for k in range(1, E):
+        for h in range(kvl):
+            if h or k == E - 1:
+                send(k, h)
+
+    def take_across(o, h):
+        all_of(nbuf.at[:, part(h)], n_recv.at[h]).wait()
+        rows = nbuf[:, h * hw:(h + 1) * hw]
+        for j in range(1, E // 2):
+            to = side * (E // 2) + lax.rem(e + j, E // 2)
+            fwd[j - 1, :, h * hw:(h + 1) * hw] = dot(sel_ref[to], rows).astype(BF16)
+            remote(fwd.at[j - 1, :, part(h)], xbuf.at[0, o, :, part(h)],
+                   z_send.at[2], z_recv.at[o, h], s, to).start()
+        xbuf[0, o, :, h * hw:(h + 1) * hw] = dot(sel_ref[e], rows).astype(BF16)
 
     def squares(g, o):
         xf = xbuf[g, o].astype(F32)
         return jnp.sum(xf * xf, axis=-1, keepdims=True)
 
-    w_copy(0).wait()
+    square_ref[...] = jnp.zeros_like(square_ref)
+
+    def gather(g, k):
+        o = origin[k]
+        for h in range(kvl):
+            if g:
+                all_of(xbuf.at[g, o, :, part(h)], x_recv.at[g - 1, o, h]).wait()
+            elif k:
+                def direct(o=o, h=h):
+                    all_of(xbuf.at[0, o, :, part(h)], z_recv.at[o, h]).wait()
+
+                if k == 1:
+                    pl.when(inner_dev)(functools.partial(take_across, o, h))
+                    pl.when(jnp.logical_not(inner_dev))(direct)
+                else:
+                    direct()
+                relay(xbuf.at[0, o, :, part(h)], o, h)
+        square_ref[g] += squares(g, o)
+
+    def slice_of(g, k):
+        if g == 0:
+            w_copy(k).wait()
+        o = origin[k]
+        x = xbuf[g, o]
+        for c0 in range(0, ff, tile):
+            got = dot(x, wbuf[o, :, c0:c0 + tile])
+            acc[g, :, c0:c0 + tile] = got if k == 0 else acc[g, :, c0:c0 + tile] + got
+
     xbuf[0, e] = pack[e]
-    square = squares(0, e)
-    x = xbuf[0, e]
-    for c0 in range(0, ff, tile):
-        acc[:, c0:c0 + tile] = dot(x, wbuf[e, :, c0:c0 + tile])
+    gather(0, 0)
+    slice_of(0, 0)
 
     rows_out, rows_in = E * RP, F * RB
     out_row = iota((rows_out, 1), 0)
@@ -243,8 +305,18 @@
     from_row = jnp.where(inner < F * cap, from_row, -1)
     perm = onehot(from_row == iota((rows_out, rows_in), 1))
 
-    def give_back(g, square, product):
-        factor = lax.rsqrt(square / depth + 1e-05)
+    last = list(range(max(1, E - 2), E))
+
+    def give_back(g):
+        factor = lax.rsqrt(square_ref[g] / depth + 1e-05)
+        xs = [xbuf[g, origin[k]] for k in last]
+
+        def product(cols):
+            total = dot(xs[0], wbuf[origin[last[0]], :, cols])
+            for x, k in zip(xs[1:], last[1:]):
+                total = total + dot(x, wbuf[origin[k], :, cols])
+            return total + acc[g, :, cols]
+
         to = at_s(S - g) if g else s
         half = (S - g) % S
         for st, (c0, n) in enumerate(steps):
@@ -266,34 +338,35 @@
                                b_send.at[0], b_recv.at[half, st], to, at_e(de))
                     c.start()
 
-    for k in range(1, E):
-        o = origin[k]
-        for h in range(kvl):
-            all_of(xbuf.at[0, o, :, part(h)], z_recv.at[o, h]).wait()
-            relay(xbuf.at[0, o, :, part(h)], o, h)
+    def others(k):
+        for g in range(1, S):
+            gather(g, k)
+            slice_of(g, k)
+
+    def middle():
+        for k in range(1, last[0]):
+            others(k)
+
+    for k in range(1, last[0]):
+        gather(0, k)
+        slice_of(0, k)
+        if k == 1:
+            others(0)
+    if last[0] == 1:
+        others(0)
+    pl.when(jnp.logical_not(inner_dev))(middle)
+    for k in last[:-1]:
+        gather(0, k)
+    gather(0, last[-1])
+    for k in last:
         w_copy(k).wait()
-        square = square + squares(0, o)
-        x = xbuf[0, o]
-        if k < E - 1:
-            for c0 in range(0, ff, tile):
-                acc[:, c0:c0 + tile] += dot(x, wbuf[o, :, c0:c0 + tile])
-        else:
-            give_back(0, square, lambda cols: acc[:, cols] + dot(x, wbuf[o, :, cols]))
-
+    pl.when((s == 0) | jnp.logical_not(inner_dev))(functools.partial(give_back, 0))
+    pl.when(inner_dev)(middle)
     for g in range(1, S):
-        square = jnp.zeros((RB, 1), F32)
-        for o in range(E):
-            for h in range(kvl):
-                all_of(xbuf.at[g, o, :, part(h)], x_recv.at[g - 1, o, h]).wait()
-            square = square + squares(g, o)
-
-        def whole(cols, g=g):
-            total = dot(xbuf[g, 0], wbuf[0, :, cols])
-            for o in range(1, E):
-                total = total + dot(xbuf[g, o], wbuf[o, :, cols])
-            return total
-
-        give_back(g, square, whole)
+        for k in last:
+            gather(g, k)
+        give_back(g)
+    pl.when((s > 0) & inner_dev)(functools.partial(give_back, 0))
 
     ins[5].wait()
     diagonal = iota((T, T), 0) == iota((T, T), 1)
@@ -333,7 +406,18 @@
             lo, n = spans[i]
             all_of(kvbuf.at[:, :, pl.ds(lo, n)], kv_send.at[i]).wait()
     all_of(rbuf.at[pl.ds(1, E - 1)], r_send.at[0]).wait()
-    all_of(pack.at[pl.ds(0, E - 1)], z_send.at[0]).wait()
+
+    @pl.when(jnp.logical_not(inner_dev))
+    def _():
+        all_of(pack.at[pl.ds(0, E - 1)], z_send.at[0]).wait()
+
+    @pl.when(inner_dev)
+    def _():
+        all_of(raw, z_send.at[1]).wait()
+        if E > 2:
+            all_of(pack.at[pl.ds(0, E // 2 - 1)], z_send.at[0]).wait()
+            all_of(fwd, z_send.at[2]).wait()
+
     all_of(xbuf.at[pl.ds(0, S - 1)], x_send.at[0]).wait()
     all_of(sendbuf.at[pl.ds(0, S * E - 1)], b_send.at[0]).wait()
 
@@ -383,9 +467,14 @@
             pltpu.VMEM((E, width, ff), BF16),
             pltpu.VMEM((kvl, 2, kv_rows, HD), BF16),
             pltpu.VMEM((E, 2, T), jnp.int32),
+            pltpu.VMEM(queries.shape, BF16),
+            pltpu.VMEM(queries.shape, BF16),
+            pltpu.VMEM((max(1, E // 2 - 1), RB, width), BF16),
+            pltpu.VMEM((E, RB, q_rows), BF16),
             pltpu.VMEM((E, RB, width), BF16),
             pltpu.VMEM((S, E, RB, width), BF16),
-            pltpu.VMEM((RB, ff), F32),
+            pltpu.VMEM((S, RB, ff), F32),
+            pltpu.VMEM((S, RB, 1), F32),
             pltpu.VMEM((S * E, RP, nc), BF16),
             pltpu.VMEM((S, E, RP, nc), BF16),
             dma((6,)),
@@ -393,9 +482,9 @@
             dma((len(pieces),)),
             dma((len(pieces), kvl)),
             dma((1,)), dma((1,)),
-            dma((1,)), dma((E, kvl)),
+            dma((3,)), dma((E, kvl)),
             dma((1,)), dma((S - 1, E, kvl)),
-            dma((1,)), dma((S, len(steps))),
+            dma((1,)), dma((S, len(steps))), dma((kvl,)),
         ],
         compiler_params=pltpu.CompilerParams(
             collective_id=0, has_side_effects=True, vmem_limit_bytes=60 * 1024 * 1024

time: 36.1 us -> 34.4 us (0.953)
  the two profiles are of different devices: /device:TPU:0 before, /device:TPU:2 now
where the time goes in v3:
time: 34.4 us; the launch traced here: 34.3 us
  Pallas kernels  33.6 us (98%)
  local copies, waits for them, and re-layouts  0.69 us (2%)
    pallas_call x1, Pallas kernels, shards(): pl.pallas_call(functools.partial(kernel, cfg), out_shape=pltpu.VMEM((T, S...  33.6 us
    unnamed x1, local copies, waits for them, and re-layouts  0.69 us

profile of v3, /device:TPU:2, one launch (start us, length us, event | category | flops | bytes accessed | tf_op | source)
XLA Modules:
  0.0 34.3 jit_solution(15115447064971443069)
XLA Ops:
  0.0 33.6 %shard_map.73 = bf16[16,7168]{1,0:T(8,128)(2,1)S(1)} custom-call(s32[8]{0:T(128)} %len_hbm.1, bf16[64,1024]{1,0:T(8,128)(2,1)} %q_hbm.1, bf16[256,256]{1,0:T(8,128)(2,1)} %k_hbm.1, bf16[256,256]{1,0:T(8,128)(2,1)} %v_hbm.1, s32[2,16]{1,0:T(2,128)} %bitcast.4, f32[2,16]{1,0:T(2,128)} %bitcast.5, bf16[4096,3584]{1,0:T(8,128)(2,1)} %bitcast.3), custom_call_target="tpu_custom_call" | custom-call | tf_op jit(solution)/shard_map/pallas_call | solution.py:455
  33.6 0.7 %copy.9 = bf16[16,7168]{1,0:T(8,128)(2,1)} copy(bf16[16,7168]{1,0:T(8,128)(2,1)S(1)} %shard_map.73) | data formatting | bytes 458752

commit v4 on v3

--- a/solution.py
+++ b/solution.py
@@ -291,11 +291,10 @@
         x = xbuf[g, o]
         for c0 in range(0, ff, tile):
             got = dot(x, wbuf[o, :, c0:c0 + tile])
-            acc[g, :, c0:c0 + tile] = got if k == 0 else acc[g, :, c0:c0 + tile] + got
+            acc[g, :, c0:c0 + tile] += got
 
     xbuf[0, e] = pack[e]
     gather(0, 0)
-    slice_of(0, 0)
 
     rows_out, rows_in = E * RP, F * RB
     out_row = iota((rows_out, 1), 0)
@@ -343,17 +342,36 @@
             gather(g, k)
             slice_of(g, k)
 
+    def own_slices(first):
+        for g in range(1, S):
+            gather(g, 0)
+        w_copy(0).wait()
+        x = jnp.concatenate([xbuf[g, e] for g in range(S)], axis=0)
+        for c0 in range(0, ff, tile):
+            got = dot(x, wbuf[e, :, c0:c0 + tile])
+            for g in range(S):
+                block = got[g * RB:(g + 1) * RB]
+                if first or g:
+                    acc[g, :, c0:c0 + tile] = block
+                else:
+                    acc[g, :, c0:c0 + tile] += block
+
     def middle():
         for k in range(1, last[0]):
             others(k)
 
     for k in range(1, last[0]):
         gather(0, k)
-        slice_of(0, k)
         if k == 1:
-            others(0)
+            w_copy(k).wait()
+            o = origin[k]
+            for c0 in range(0, ff, tile):
+                acc[0, :, c0:c0 + tile] = dot(xbuf[0, o], wbuf[o, :, c0:c0 + tile])
+            own_slices(False)
+        else:
+            slice_of(0, k)
     if last[0] == 1:
-        others(0)
+        own_slices(True)
     pl.when(jnp.logical_not(inner_dev))(middle)
     for k in last[:-1]:
         gather(0, k)
@@ -387,17 +405,23 @@
     )
     g0, g1 = column(gates_ref[0:1, :]), column(gates_ref[1:2, :])
 
-    for half in range(S):
-        base = lax.rem(s + half, S) * ff
+    for owner in range(S):
+        half = lax.rem(owner + S - s, S)
         for st, (c0, n) in enumerate(steps):
-            came = recv.at[half, pl.ds(0 if half else 1, E if half else E - 1), :, pl.ds(c0, n)]
-            all_of(came, b_recv.at[half, st]).wait()
+            @pl.when(s == owner)
+            def _():
+                all_of(recv.at[0, pl.ds(1, E - 1), :, pl.ds(c0, n)], b_recv.at[0, st]).wait()
+
+            @pl.when(s != owner)
+            def _():
+                all_of(recv.at[half, :, :, pl.ds(c0, n)], b_recv.at[half, st]).wait()
+
             got = recv[half, :, :, c0:c0 + n].reshape(E * RP, n)
             res = dot(pick, got)
             for f in range(F):
                 lo = 2 * f * T
                 mix = g0 * res[lo:lo + T] + g1 * res[lo + T:lo + 2 * T]
-                cols = pl.ds(pl.multiple_of(base + f * nc + c0, 128), n)
+                cols = slice(owner * ff + f * nc + c0, owner * ff + f * nc + c0 + n)
                 out_ref[:, cols] = mix.astype(BF16)
 
     for i, (d, first) in enumerate(pieces):

time: 34.4 us -> 33.8 us (0.983)
  the two profiles are of different devices: /device:TPU:2 before, /device:TPU:0 now
where the time goes in v4:
time: 33.8 us; the launch traced here: 33.6 us
  Pallas kernels  32.9 us (97%)
  local copies, waits for them, and re-layouts  0.69 us (2%)
    pallas_call x1, Pallas kernels, shards(): pl.pallas_call(functools.partial(kernel, cfg), out_shape=pltpu.VMEM((T, S...  32.9 us
    unnamed x1, local copies, waits for them, and re-layouts  0.69 us

profile of v4, /device:TPU:0, one launch (start us, length us, event | category | flops | bytes accessed | tf_op | source)
XLA Modules:
  0.0 33.6 jit_solution(13531573586660751300)
XLA Ops:
  0.0 32.9 %shard_map.73 = bf16[16,7168]{1,0:T(8,128)(2,1)S(1)} custom-call(s32[8]{0:T(128)} %len_hbm.1, bf16[64,1024]{1,0:T(8,128)(2,1)} %q_hbm.1, bf16[256,256]{1,0:T(8,128)(2,1)} %k_hbm.1, bf16[256,256]{1,0:T(8,128)(2,1)} %v_hbm.1, s32[2,16]{1,0:T(2,128)} %bitcast.4, f32[2,16]{1,0:T(2,128)} %bitcast.5, bf16[4096,3584]{1,0:T(8,128)(2,1)} %bitcast.3), custom_call_target="tpu_custom_call" | custom-call | tf_op jit(solution)/shard_map/pallas_call | solution.py:479
  32.9 0.7 %copy.9 = bf16[16,7168]{1,0:T(8,128)(2,1)} copy(bf16[16,7168]{1,0:T(8,128)(2,1)S(1)} %shard_map.73) | data formatting | bytes 458752

commit v5 on v4

--- a/solution.py
+++ b/solution.py
@@ -36,11 +36,14 @@
     len_ref, q_ref, k_ref, v_ref, routes_ref, gates_ref,
     wbuf, kvbuf, rbuf, raw, nbuf, fwd, sel_ref, pack, xbuf, acc, square_ref, sendbuf, recv,
     in_sem, w_sem, kv_send, kv_recv, r_send, r_recv, z_send, z_recv, x_send, x_recv,
-    b_send, b_recv, n_recv,
+    b_send, b_recv, n_recv, turn,
 ):
     S, E, ndoc, cap, RB, F, RP, nc, steps, pieces, tile = cfg
     s = lax.axis_index("seq")
     e = lax.axis_index("expert")
+    dp = lax.axis_index("dp")
+    core = lax.rem(dp, 2)
+    partner = {"dp": dp + 1 - 2 * core}
     Q, width = q_ref.shape
     shard = k_ref.shape[0]
     kvl = k_ref.shape[1] // HD
@@ -65,6 +68,8 @@
                     barrier, inc=1, device_id={"seq": at_s(ds), "expert": at_e(de)},
                     device_id_type=MESH,
                 )
+
+    pl.semaphore_signal(barrier, inc=1, device_id=partner, device_id_type=MESH)
 
     mid = (E // 2 - 1, E // 2)
 
@@ -125,6 +130,29 @@
         kpos = first + iota((1, k.shape[0]), 1)
         return jnp.where((kpos <= qpos) & (kpos >= docstart), sc, F32(-1e30))
 
+    spans = []
+    offset = 0
+    for d, first in pieces:
+        spans.append((offset, shard - first))
+        offset += shard - first
+
+    def greet():
+        pl.semaphore_wait(barrier, S + E - 1)
+        for h in range(kvl):
+            for i, (d, first) in enumerate(pieces):
+                @pl.when(s + d < S)
+                def _():
+                    lo, n = spans[i]
+                    for j, ref in enumerate((k_ref, v_ref)):
+                        remote(
+                            ref.at[pl.ds(first, n), pl.ds(h * HD, HD)],
+                            kvbuf.at[h, j, pl.ds(lo, n)],
+                            kv_send.at[i], kv_recv.at[i, h], s + d, e,
+                        ).start()
+        for de in range(1, E):
+            remote(routes_ref, rbuf.at[de], r_send.at[0], r_recv.at[0], s, at_e(de)).start()
+
+    pl.when(e > 0)(greet)
     queries = []
     local = []
     for h in range(kvl):
@@ -138,26 +166,7 @@
         local.append((peak, jnp.sum(wt, axis=-1, keepdims=True),
                       dot(wt.astype(BF16), v_ref[:, h * HD:(h + 1) * HD])))
 
-    pl.semaphore_wait(barrier, S + E - 2)
-
-    spans = []
-    offset = 0
-    for d, first in pieces:
-        spans.append((offset, shard - first))
-        offset += shard - first
-    for h in range(kvl):
-        for i, (d, first) in enumerate(pieces):
-            @pl.when(s + d < S)
-            def _():
-                lo, n = spans[i]
-                for j, ref in enumerate((k_ref, v_ref)):
-                    remote(
-                        ref.at[pl.ds(first, n), pl.ds(h * HD, HD)],
-                        kvbuf.at[h, j, pl.ds(lo, n)],
-                        kv_send.at[i], kv_recv.at[i, h], s + d, e,
-                    ).start()
-    for de in range(1, E):
-        remote(routes_ref, rbuf.at[de], r_send.at[0], r_recv.at[0], s, at_e(de)).start()
+    pl.when(e == 0)(greet)
 
     def part(h):
         return pl.ds(h * hw, hw)
@@ -182,6 +191,33 @@
     def _():
         for h in range(kvl):
             store_head(h, local[h][2], local[h][1])
+
+    for h in range(kvl):
+        peak, total, got = local[h]
+
+        @pl.when(s > 0)
+        def _():
+            q = queries[h]
+            run_peak, run_total, run_got = peak, total, got
+            for i, (d, first) in enumerate(pieces):
+                lo, n = spans[i]
+                if d > 1:
+                    @pl.when(s < d)
+                    def _():
+                        kvbuf[h, :, lo:lo + n] = jnp.zeros((2, n, HD), BF16)
+
+                @pl.when(s >= d)
+                def _():
+                    all_of(kvbuf.at[h, :, pl.ds(lo, n)], kv_recv.at[i, h]).wait()
+
+                sc = masked(q, kvbuf[h, 0, lo:lo + n], (s - d) * shard + first)
+                higher = jnp.maximum(run_peak, jnp.max(sc, axis=-1, keepdims=True))
+                wt = jnp.exp(sc - higher)
+                fade = jnp.exp(run_peak - higher)
+                run_total = run_total * fade + jnp.sum(wt, axis=-1, keepdims=True)
+                run_got = run_got * fade + dot(wt.astype(BF16), kvbuf[h, 1, lo:lo + n])
+                run_peak = higher
+            store_head(h, run_got, run_total)
 
     all_of(rbuf.at[pl.ds(1, E - 1)], r_recv.at[0]).wait()
     mine = routes_ref[...]
@@ -213,32 +249,6 @@
                    z_send.at[0], z_recv.at[e, h], s, to).start()
 
     for h in range(kvl):
-        peak, total, got = local[h]
-
-        @pl.when(s > 0)
-        def _():
-            q = queries[h]
-            run_peak, run_total, run_got = peak, total, got
-            for i, (d, first) in enumerate(pieces):
-                lo, n = spans[i]
-                if d > 1:
-                    @pl.when(s < d)
-                    def _():
-                        kvbuf[h, :, lo:lo + n] = jnp.zeros((2, n, HD), BF16)
-
-                @pl.when(s >= d)
-                def _():
-                    all_of(kvbuf.at[h, :, pl.ds(lo, n)], kv_recv.at[i, h]).wait()
-
-                sc = masked(q, kvbuf[h, 0, lo:lo + n], (s - d) * shard + first)
-                higher = jnp.maximum(run_peak, jnp.max(sc, axis=-1, keepdims=True))
-                wt = jnp.exp(sc - higher)
-                fade = jnp.exp(run_peak - higher)
-                run_total = run_total * fade + jnp.sum(wt, axis=-1, keepdims=True)
-                run_got = run_got * fade + dot(wt.astype(BF16), kvbuf[h, 1, lo:lo + n])
-                run_peak = higher
-            store_head(h, run_got, run_total)
-
         packed = dot(selector, raw[:, h * hw:(h + 1) * hw]).astype(BF16)
         for x in range(E):
             pack[x, :, h * hw:(h + 1) * hw] = packed[x * RB:(x + 1) * RB]
@@ -378,13 +388,32 @@
     gather(0, last[-1])
     for k in last:
         w_copy(k).wait()
-    pl.when((s == 0) | jnp.logical_not(inner_dev))(functools.partial(give_back, 0))
+    def hand():
+        @pl.when(core == 0)
+        def _():
+            pl.semaphore_signal(turn.at[0], inc=1, device_id=partner, device_id_type=MESH)
+
+        @pl.when(core == 1)
+        def _():
+            pl.semaphore_wait(turn.at[0], 1)
+
+    late = (s > 0) & inner_dev
+
+    @pl.when(jnp.logical_not(late))
+    def _():
+        give_back(0)
+        hand()
+
     pl.when(inner_dev)(middle)
     for g in range(1, S):
         for k in last:
             gather(g, k)
         give_back(g)
-    pl.when((s > 0) & inner_dev)(functools.partial(give_back, 0))
+
+    @pl.when(late)
+    def _():
+        hand()
+        give_back(0)
 
     ins[5].wait()
     diagonal = iota((T, T), 0) == iota((T, T), 1)
@@ -509,6 +538,7 @@
             dma((3,)), dma((E, kvl)),
             dma((1,)), dma((S - 1, E, kvl)),
             dma((1,)), dma((S, len(steps))), dma((kvl,)),
+            pltpu.SemaphoreType.REGULAR((1,)),
         ],
         compiler_params=pltpu.CompilerParams(
             collective_id=0, has_side_effects=True, vmem_limit_bytes=60 * 1024 * 1024

time: 33.8 us -> 33 us (0.976)
  Pallas kernels: 32.9 us -> 32.1 us
    pallas_call x1, Pallas kernels: 32.9 us -> 32.1 us  [shards(): pl.pallas_call(functools.partial(kernel, cfg), out_shape=pltpu.VMEM((T, S...]
where the time goes in v5:
time: 33 us; the launch traced here: 32.8 us
  Pallas kernels  32.1 us (97%)
  local copies, waits for them, and re-layouts  0.69 us (2%)
    pallas_call x1, Pallas kernels, shards(): pl.pallas_call(functools.partial(kernel, cfg), out_shape=pltpu.VMEM((T, S...  32.1 us
    unnamed x1, local copies, waits for them, and re-layouts  0.69 us

profile of v5, /device:TPU:0, one launch (start us, length us, event | category | flops | bytes accessed | tf_op | source)
XLA Modules:
  0.0 32.8 jit_solution(8227782486430177281)
XLA Ops:
  0.0 32.1 %shard_map.73 = bf16[16,7168]{1,0:T(8,128)(2,1)S(1)} custom-call(s32[8]{0:T(128)} %len_hbm.1, bf16[64,1024]{1,0:T(8,128)(2,1)} %q_hbm.1, bf16[256,256]{1,0:T(8,128)(2,1)} %k_hbm.1, bf16[256,256]{1,0:T(8,128)(2,1)} %v_hbm.1, s32[2,16]{1,0:T(2,128)} %bitcast.4, f32[2,16]{1,0:T(2,128)} %bitcast.5, bf16[4096,3584]{1,0:T(8,128)(2,1)} %bitcast.3), custom_call_target="tpu_custom_call" | custom-call | tf_op jit(solution)/shard_map/pallas_call | solution.py:508
  32.1 0.7 %copy.9 = bf16[16,7168]{1,0:T(8,128)(2,1)} copy(bf16[16,7168]{1,0:T(8,128)(2,1)S(1)} %shard_map.73) | data formatting | bytes 458752

commit v6 on v5

--- a/solution.py
+++ b/solution.py
@@ -173,7 +173,7 @@
 
     def relay(src, o, h):
         for ds in range(1, S):
-            remote(src, xbuf.at[ds, o, :, part(h)], x_send.at[0], x_recv.at[ds - 1, o, h],
+            remote(src, xbuf.at[ds, o, :, part(h)], x_send.at[0], x_recv.at[ds - 1, o],
                    at_s(ds), e).start()
 
     def store_head(h, got, total):
@@ -279,10 +279,10 @@
 
     def gather(g, k):
         o = origin[k]
+        if g:
+            all_of(xbuf.at[g, o], x_recv.at[g - 1, o]).wait()
         for h in range(kvl):
-            if g:
-                all_of(xbuf.at[g, o, :, part(h)], x_recv.at[g - 1, o, h]).wait()
-            elif k:
+            if k and not g:
                 def direct(o=o, h=h):
                     all_of(xbuf.at[0, o, :, part(h)], z_recv.at[o, h]).wait()
 
@@ -316,7 +316,18 @@
 
     last = list(range(max(1, E - 2), E))
 
-    def give_back(g):
+    def hand():
+        @pl.when(core == 0)
+        def _():
+            pl.semaphore_signal(turn.at[0], inc=1, device_id=partner, device_id_type=MESH)
+
+        @pl.when(core == 1)
+        def _():
+            pl.semaphore_wait(turn.at[0], 1)
+
+    late = (s > 0) & inner_dev
+
+    def give_back(g, leads=None):
         factor = lax.rsqrt(square_ref[g] / depth + 1e-05)
         xs = [xbuf[g, origin[k]] for k in last]
 
@@ -346,6 +357,8 @@
                                recv.at[half, de, :, pl.ds(c0, n)],
                                b_send.at[0], b_recv.at[half, st], to, at_e(de))
                     c.start()
+            if leads is not None and st == 1:
+                pl.when(leads & (core == 0))(hand)
 
     def others(k):
         for g in range(1, S):
@@ -388,31 +401,21 @@
     gather(0, last[-1])
     for k in last:
         w_copy(k).wait()
-    def hand():
-        @pl.when(core == 0)
-        def _():
-            pl.semaphore_signal(turn.at[0], inc=1, device_id=partner, device_id_type=MESH)
-
-        @pl.when(core == 1)
-        def _():
-            pl.semaphore_wait(turn.at[0], 1)
-
-    late = (s > 0) & inner_dev
 
     @pl.when(jnp.logical_not(late))
     def _():
-        give_back(0)
-        hand()
+        give_back(0, s >= 0)
+        pl.when(core == 1)(hand)
 
     pl.when(inner_dev)(middle)
     for g in range(1, S):
         for k in last:
             gather(g, k)
-        give_back(g)
+        give_back(g, late if g == S - 1 else None)
 
     @pl.when(late)
     def _():
-        hand()
+        pl.when(core == 1)(hand)
         give_back(0)
 
     ins[5].wait()
@@ -536,7 +539,7 @@
             dma((len(pieces), kvl)),
             dma((1,)), dma((1,)),
             dma((3,)), dma((E, kvl)),
-            dma((1,)), dma((S - 1, E, kvl)),
+            dma((1,)), dma((S - 1, E)),
             dma((1,)), dma((S, len(steps))), dma((kvl,)),
             pltpu.SemaphoreType.REGULAR((1,)),
         ],

time: 33 us -> 33 us (level)
  the two profiles are of different devices: /device:TPU:0 before, /device:TPU:6 now
where the time goes in v6:
time: 33 us; the launch traced here: 32.8 us
  Pallas kernels  32.1 us (97%)
  local copies, waits for them, and re-layouts  0.69 us (2%)
    pallas_call x1, Pallas kernels, shards(): pl.pallas_call(functools.partial(kernel, cfg), out_shape=pltpu.VMEM((T, S...  32.1 us
    unnamed x1, local copies, waits for them, and re-layouts  0.69 us

profile of v6, /device:TPU:6, one launch (start us, length us, event | category | flops | bytes accessed | tf_op | source)
XLA Modules:
  0.0 32.8 jit_solution(9868383355021055573)
XLA Ops:
  0.0 32.1 %shard_map.73 = bf16[16,7168]{1,0:T(8,128)(2,1)S(1)} custom-call(s32[8]{0:T(128)} %len_hbm.1, bf16[64,1024]{1,0:T(8,128)(2,1)} %q_hbm.1, bf16[256,256]{1,0:T(8,128)(2,1)} %k_hbm.1, bf16[256,256]{1,0:T(8,128)(2,1)} %v_hbm.1, s32[2,16]{1,0:T(2,128)} %bitcast.4, f32[2,16]{1,0:T(2,128)} %bitcast.5, bf16[4096,3584]{1,0:T(8,128)(2,1)} %bitcast.3), custom_call_target="tpu_custom_call" | custom-call | tf_op jit(solution)/shard_map/pallas_call | solution.py:511
  32.1 0.7 %copy.9 = bf16[16,7168]{1,0:T(8,128)(2,1)} copy(bf16[16,7168]{1,0:T(8,128)(2,1)S(1)} %shard_map.73) | data formatting | bytes 458752
